TPU v7x, 32 devices: a whole 2x2x4 slice. The times are simulated.
32 devices in a mesh: band: 8 (over y, x, core), sub: 4 (over z).
Axes of the slice: x: 2, y: 2, z: 4, core: 2. Of those that a mesh axis runs over, the one named last changes fastest.
Arguments:
- fields: bfloat16 [12, 1048576], P(None, ('band', 'sub')), may hold values from -1.5 to 6
- land_mask: int32 [1048576], P(('band', 'sub')), may hold values from 0 to 1
- intersection: bfloat16 [8192, 128, 128], P(('band', 'sub')), as said below
- send_slot: int32 [8192], P(('band', 'sub')), may hold values from 0 to 511, as said below
- target_block: int32 [8192], P(('band', 'sub')), may hold values from 0 to 15
- live_blocks: int32 [32], P(('band', 'sub')), may hold values from 192 to 256, as said below
Outputs:
- remapped: float32 [12, 65536], P(None, ('band', 'sub'))
Inputs may be any that keep to these rules, and one draw needn't show every extreme that they name: `send_slot`: within one device's 256 entries the values are distinct; value // 16 is the device that owns the block's target; in each device's entries some owner is named exactly 16 times and none more. `live_blocks`: some device has all 256 slots live in every draw. `intersection`: entries are positive.
All inputs are finite; a program needn't handle non-finite values.
Results may differ from a plain program's by a relative error of at most 0.0003.
Values may be sent and summed in bfloat16 or wider, within the bound.
A program may use at most 64 MiB of HBM per device.

v0:
```python
import functools
import itertools
import math

import jax
import jax.numpy as jnp
from jax import lax
from jax.experimental import pallas as pl
from jax.experimental.pallas import tpu as pltpu
from jax.sharding import PartitionSpec as P

TB_DEV = 16
GROUP = 16
TILE = 8
PIECES = TB_DEV // TILE
LEVELS = 32700.0


def in_hbm(a):
    return pltpu.with_memory_space_constraint(a, pltpu.HBM)


def contribute(
    capacity, rows, owners, slot_ref, target_ref, live_ref, f_hbm, m_hbm, w_hbm, acc_ref, f_all, m_all, w_all, fx, tot, top, sem
):
    field_count = f_hbm.shape[0]
    cells = w_hbm.shape[2]
    steps = f_all.shape[0]
    width = GROUP * cells

    def copies(i):
        return (
            pltpu.make_async_copy(m_hbm.at[pl.ds(i * GROUP, GROUP)], m_all.at[i], sem.at[0, i]),
            pltpu.make_async_copy(f_hbm.at[:, pl.ds(i * width, width)], f_all.at[i], sem.at[1, i]),
            pltpu.make_async_copy(w_hbm.at[pl.ds(i * GROUP, GROUP)], w_all.at[i], sem.at[2, i]),
        )

    for i in range(steps):
        for copy in copies(i):
            copy.start()
    acc_ref[...] = jnp.zeros_like(acc_ref)
    tot[...] = jnp.zeros_like(tot)
    top[...] = jnp.zeros_like(top)
    extra = lax.broadcasted_iota(jnp.int32, (fx.shape[0] - field_count, fx.shape[1]), 0)
    fx[field_count:, :] = jnp.where(extra == 0, 1.0, 0.0)
    live = live_ref[0]
    part = 16

    def step(i, carry):
        for copy in copies(i):
            copy.wait()
        fx[:field_count, :] = f_all[i].astype(jnp.float32)
        total = tot[...]
        most = top[...]
        for first in range(0, GROUP, part):
            products = []
            for j in range(first, first + part):
                b = i * GROUP + j
                kept = jnp.where(b < live, m_all[i, j : j + 1, :], 0).astype(jnp.float32)
                x = fx[:, j * cells : (j + 1) * cells] * kept
                total = total + x
                most = jnp.maximum(most, jnp.abs(x))
                products.append(
                    jnp.dot(x.astype(jnp.bfloat16), w_all[i, j], preferred_element_type=jnp.float32)
                )
            for j in range(first, first + part):
                b = i * GROUP + j
                target = target_ref[b]
                row = ((slot_ref[b] // capacity) * PIECES + target // TILE) * rows
                row = row + (target % TILE) * (field_count + 1)
                acc_ref[pl.ds(row, 16), :] += products[j - first]
        tot[...] = total
        top[...] = most
        return carry

    lax.fori_loop(0, steps, step, 0)
    total = tot[...]
    most = top[...]
    low = jnp.sum(total[:TILE], axis=1, keepdims=True)
    high = jnp.sum(total[TILE:], axis=1, keepdims=True)
    lane = lax.broadcasted_iota(jnp.int32, (TILE, cells), 1)
    row = lax.broadcasted_iota(jnp.int32, most.shape, 0)
    largest = jnp.max(jnp.where(row < field_count, most, 0.0))
    packed = jnp.where(lane == 0, low, jnp.where(lane == 1, high, largest))
    for chunk in range(owners * PIECES):
        start = (chunk + 1) * rows - TILE
        acc_ref[start : start + TILE, :] = packed


def exchange(sizes, orders, field_count, acc_ref, out_ref, *scratch):
    ny, nx, nz = sizes["y"], sizes["x"], sizes["z"]
    band, z = lax.axis_index("band"), lax.axis_index("sub")
    core = lax.rem(band, 2)
    x = lax.rem(band // 2, nx)
    y = band // (2 * nx)
    coords = {"y": y, "x": x, "z": z}

    def device(**moved):
        at = dict(coords, core=core)
        at.update(moved)
        return {"band": (at["y"] * nx + at["x"]) * 2 + at["core"], "sub": at["z"]}

    partners = [device(core=1 - core)]
    for name, size in sizes.items():
        for k in range(1, size):
            partners.append(device(**{name: lax.rem(coords[name] + k, size)}))
    barrier = pltpu.get_barrier_semaphore()
    for partner in partners:
        pl.semaphore_signal(barrier, inc=1, device_id=partner, device_id_type=pl.DeviceIdType.MESH)
    pl.semaphore_wait(barrier, len(partners))

    send_sem, recv_sem = scratch[-2:]
    buffers = iter(scratch[:-2])
    cells = acc_ref.shape[-1]
    lane = lax.broadcasted_iota(jnp.int32, (TILE, cells), 1)
    packed_rows = field_count * TILE
    counter = [0]
    started = []

    def send(src, dst, partner):
        k = counter[0]
        counter[0] += 1
        copy = pltpu.make_async_remote_copy(
            src_ref=src,
            dst_ref=dst,
            send_sem=send_sem.at[k],
            recv_sem=recv_sem.at[k],
            device_id=partner,
            device_id_type=pl.DeviceIdType.MESH,
        )
        copy.start()
        started.append(copy)
        return copy

    def merge(a, b):
        return jnp.where(lane < 2, a + b, jnp.maximum(a, b))

    def encode(sums, at, gain, codes, heads, to):
        fraction = sums[(*at, slice(packed_rows, packed_rows + TILE))]
        gain = jnp.where(fraction > 0.0, 1.0 / fraction, 0.0) * gain
        for f in range(0, field_count, 2):
            first = sums[(*at, slice(f * TILE, (f + 1) * TILE))] * gain
            second = sums[(*at, slice((f + 1) * TILE, (f + 2) * TILE))] * gain
            pair = jnp.concatenate([first, second], axis=0)
            code = jnp.round(pair).astype(jnp.int32).astype(jnp.int16)
            codes[(*to, slice(f * TILE, (f + 2) * TILE))] = code
        heads[to] = fraction

    def decode(codes, heads, at, gain):
        fraction = heads[at]
        gain = fraction * gain
        tiles = []
        for f in range(0, field_count, 2):
            code = codes[(*at, slice(f * TILE, (f + 2) * TILE))]
            pair = code.astype(jnp.int32).astype(jnp.float32)
            tiles += [pair[:TILE] * gain, pair[TILE:] * gain]
        return tiles + [fraction]

    class Piece:
        pass

    pieces = []
    for p, order in enumerate(orders):
        piece = Piece()
        piece.order, piece.left = order, ["y", "x", "z"]
        piece.landed, piece.sums = next(buffers), next(buffers)
        piece.steps = [[next(buffers) for _ in range(7)] for _ in order]
        src = acc_ref.at[:, :, 1 - core, :, p]
        piece.pending = [send(src, piece.landed, device(core=1 - core))]
        pieces.append(piece)

    def launch(piece, phase):
        name = piece.order[phase]
        axis = piece.left.index(name)
        out_codes, out_heads, out_extra, in_codes, in_heads, in_extra, _ = piece.steps[phase]
        out_extra[...] = piece.extra
        largest = piece.extra[:, 2:3]
        gain = jnp.where(largest > 0.0, LEVELS / jnp.maximum(largest, 1e-30), 0.0)
        rest = [sizes[d] for d in piece.left if d != name]
        piece.pending = []
        for k in range(1, sizes[name]):
            peer = lax.rem(coords[name] + k, sizes[name])
            for at in itertools.product(*[range(n) for n in rest]):
                encode(piece.sums, (*at[:axis], peer, *at[axis:]), gain, out_codes, out_heads, (k - 1, *at))
            to = device(**{name: peer})
            piece.pending.append(
                (
                    send(out_codes.at[k - 1], in_codes.at[k - 1], to),
                    send(out_heads.at[k - 1], in_heads.at[k - 1], to),
                    send(out_extra, in_extra.at[k - 1], to),
                )
            )

    def collect(piece, phase):
        name = piece.order[phase]
        axis = piece.left.index(name)
        _, _, _, in_codes, in_heads, in_extra, after = piece.steps[phase]
        rest = [sizes[d] for d in piece.left if d != name]
        for copies in piece.pending:
            for copy in copies:
                copy.wait_recv()
        extras = [in_extra[k - 1] for k in range(1, sizes[name])]
        piece.extra = functools.reduce(merge, extras, piece.extra)
        gains = [extra[:, 2:3] * (1.0 / LEVELS) for extra in extras]
        for at in itertools.product(*[range(n) for n in rest]):
            own = (*at[:axis], coords[name], *at[axis:])
            tiles = [
                piece.sums[(*own, slice(f * TILE, (f + 1) * TILE))] for f in range(field_count + 1)
            ]
            for k in range(1, sizes[name]):
                more = decode(in_codes, in_heads, (k - 1, *at), gains[k - 1])
                tiles = [a + b for a, b in zip(tiles, more)]
            for f, tile in enumerate(tiles):
                after[(*at, slice(f * TILE, (f + 1) * TILE))] = tile
        piece.left.remove(name)
        piece.sums = after

    for p, piece in enumerate(pieces):
        piece.pending[0].wait_recv()
        for yi, xi, zi in itertools.product(range(ny), range(nx), range(nz)):
            for f in range(field_count + 1):
                strided = pl.ds(f, TILE, stride=field_count + 1)
                tile = acc_ref[yi, xi, core, zi, p, strided, :] + piece.landed[yi, xi, zi, strided, :]
                piece.sums[yi, xi, zi, f * TILE : (f + 1) * TILE, :] = tile
        extra = slice(packed_rows + TILE, packed_rows + 2 * TILE)
        piece.extra = merge(acc_ref[0, 0, core, 0, p, extra, :], piece.landed[0, 0, 0, extra, :])
        launch(piece, 0)
    for phase in range(3):
        for piece in pieces:
            collect(piece, phase)
            if phase < 2:
                launch(piece, phase + 1)

    totals = pieces[0].extra
    row, column = field_count % TILE, field_count // TILE
    count = jnp.maximum(totals[row : row + 1, column : column + 1], 1.0)
    means = totals / count
    for p, piece in enumerate(pieces):
        fraction = piece.sums[packed_rows : packed_rows + TILE, :]
        short = jnp.maximum(0.25 - fraction, 0.0)
        least = jnp.maximum(fraction, 0.25)
        for f in range(field_count):
            row, column = f % TILE, f // TILE
            mean = means[row : row + 1, column : column + 1]
            numer = piece.sums[f * TILE : (f + 1) * TILE, :]
            out_ref[f, p * TILE : (p + 1) * TILE, :] = (numer + short * mean) / least
    for copy in started:
        copy.wait_send()


def body(sizes, fields, land_mask, intersection, send_slot, target_block, live_blocks):
    block_count, cells = intersection.shape[0], intersection.shape[1]
    field_count = fields.shape[0]
    nx, ny, nz = sizes["x"], sizes["y"], sizes["z"]
    owners = ny * nx * 2 * nz
    capacity = max(2, 2 * block_count // owners)
    rows = (field_count + 2) * TILE
    steps = block_count // GROUP
    smem = pl.BlockSpec(memory_space=pltpu.SMEM)
    acc = pl.pallas_call(
        functools.partial(contribute, capacity, rows, owners),
        in_specs=[smem, smem, smem] + [pl.BlockSpec(memory_space=pltpu.HBM)] * 3,
        out_specs=pl.BlockSpec(memory_space=pltpu.VMEM),
        out_shape=jax.ShapeDtypeStruct((owners * PIECES * rows, cells), jnp.float32),
        scratch_shapes=[
            pltpu.VMEM((steps, field_count, GROUP * cells), jnp.bfloat16),
            pltpu.VMEM((steps, GROUP, cells), jnp.int32),
            pltpu.VMEM((steps, GROUP, cells, cells), jnp.bfloat16),
            pltpu.VMEM((16, GROUP * cells), jnp.float32),
            pltpu.VMEM((16, cells), jnp.float32),
            pltpu.VMEM((16, cells), jnp.float32),
            pltpu.SemaphoreType.DMA((3, steps)),
        ],
        compiler_params=pltpu.CompilerParams(
            vmem_limit_bytes=40 * 2**20
        ),
    )(
        in_hbm(send_slot),
        in_hbm(target_block),
        live_blocks,
        in_hbm(fields),
        in_hbm(land_mask.reshape(block_count, cells)),
        in_hbm(intersection),
    )
    acc = acc.reshape(ny, nx, 2, nz, PIECES, rows, cells)

    orders = (("x", "y", "z"), ("y", "z", "x"))
    scratch = []
    copies = 0
    for order in orders:
        left = ["y", "x", "z"]
        shape = [sizes[d] for d in left]
        scratch.append(pltpu.VMEM((*shape, rows, cells), jnp.float32))
        scratch.append(pltpu.VMEM((*shape, rows - TILE, cells), jnp.float32))
        copies += 1
        for name in order:
            del shape[left.index(name)]
            left.remove(name)
            sent = (sizes[name] - 1, *shape)
            codes = pltpu.VMEM((*sent, field_count * TILE, cells), jnp.int16)
            heads = pltpu.VMEM((*sent, TILE, cells), jnp.float32)
            scratch += [codes, heads, pltpu.VMEM((TILE, cells), jnp.float32)]
            scratch += [codes, heads, pltpu.VMEM((sizes[name] - 1, TILE, cells), jnp.float32)]
            scratch.append(pltpu.VMEM((*shape, rows - TILE, cells), jnp.float32))
            copies += 3 * (sizes[name] - 1)
    scratch += [pltpu.SemaphoreType.DMA((copies,))] * 2
    remapped = pl.pallas_call(
        functools.partial(exchange, sizes, orders, field_count),
        in_specs=[pl.BlockSpec(memory_space=pltpu.VMEM)],
        out_specs=pl.BlockSpec(memory_space=pltpu.VMEM),
        out_shape=jax.ShapeDtypeStruct((field_count, TB_DEV, cells), jnp.float32),
        scratch_shapes=scratch,
        compiler_params=pltpu.CompilerParams(
            collective_id=0, has_side_effects=True, vmem_limit_bytes=50 * 2**20
        ),
    )(acc)
    return remapped.reshape(field_count, TB_DEV * cells)


def solution(mesh):
    band, sub = mesh.shape["band"], mesh.shape["sub"]
    plane = band // 2
    nx = max(d for d in range(1, math.isqrt(plane) + 1) if plane % d == 0)
    sizes = {"y": plane // nx, "x": nx, "z": sub}
    return jax.shard_map(
        functools.partial(body, sizes),
        mesh=mesh,
        in_specs=(
            P(None, ("band", "sub")),
            P(("band", "sub")),
            P(("band", "sub"), None, None),
            P(("band", "sub")),
            P(("band", "sub")),
            P(("band", "sub")),
        ),
        out_specs=P(None, ("band", "sub")),
        check_vma=False,
    )
```

profile of v0, /device:TPU:0, one launch (start us, length us, event | category | flops | bytes accessed | tf_op | source)
XLA Modules:
  0.0 35.3 jit_solution(9612062284094532745)
XLA Ops:
  0.7 6.7 %shard_map.64 = f32[7168,128]{1,0:T(8,128)S(1)} custom-call(s32[256]{0:T(256)} %slot_ref.1, s32[256]{0:T(256)} %target_ref.1, s32[1]{0:T(128)S(6)} %copy.8.live_ref, bf16[12,32768]{1,0:T(8,128)(2,1)} %f_hbm.1, s32[256,128]{1,0:T(8,128)} %bitcast.7, bf16[256,128,128]{2,1,0:T(8,128)(2,1)} %w_hbm.1), custom_call_target="tpu_custom_call" | custom-call | tf_op jit(solution)/shard_map/pallas_call | solution.py:260
  7.4 27.1 %shard_map.65 = f32[12,16,128]{2,1,0:T(8,128)S(1)} custom-call(f32[2,2,2,4,2,112,128]{6,5,4,3,2,1,0:T(8,128)S(1)} %bitcast.5), custom_call_target="tpu_custom_call" | custom-call | tf_op jit(solution)/shard_map/pallas_call | solution.py:307
  34.6 0.7 %copy.7 = f32[2,8,16,128]{3,1,2,0:T(8,128)} copy(f32[2,8,16,128]{3,2,1,0:T(8,128)S(1)} %bitcast.6) | data formatting | bytes 262144
  (1 shorter events, 0.0 us)
where the time goes:
time: 35.5 us; the launch traced here: 35.3 us
  Pallas kernels  33.9 us (95%)
  local copies, waits for them, and re-layouts  0.71 us (2%)
  between operations  0.68 us (2%)
    pallas_call x1, Pallas kernels, body(): pl.pallas_call(functools.partial(exchange, sizes, orders, field_count), i...  27.1 us
    pallas_call x1, Pallas kernels, body(): pl.pallas_call(functools.partial(contribute, capacity, rows, owners), in_...  6.74 us

commit v1 on v0

--- a/solution.py
+++ b/solution.py
@@ -20,8 +20,15 @@
     return pltpu.with_memory_space_constraint(a, pltpu.HBM)
 
 
+def split(value, size):
+    if size & (size - 1) == 0:
+        return value >> (size.bit_length() - 1), value & (size - 1)
+    return lax.div(value, size), lax.rem(value, size)
+
+
 def contribute(
-    capacity, rows, owners, slot_ref, target_ref, live_ref, f_hbm, m_hbm, w_hbm, acc_ref, f_all, m_all, w_all, fx, tot, top, sem
+    capacity, rows, owners, slot_hbm, target_hbm, live_hbm, f_hbm, m_hbm, w_hbm, acc_ref,
+    f_all, m_all, w_all, fx, products, tot, top, slot_ref, target_ref, live_ref, sem, scalar_sem,
 ):
     field_count = f_hbm.shape[0]
     cells = w_hbm.shape[2]
@@ -35,45 +42,64 @@
             pltpu.make_async_copy(w_hbm.at[pl.ds(i * GROUP, GROUP)], w_all.at[i], sem.at[2, i]),
         )
 
+    scalars = (
+        pltpu.make_async_copy(slot_hbm, slot_ref, scalar_sem.at[0]),
+        pltpu.make_async_copy(target_hbm, target_ref, scalar_sem.at[1]),
+        pltpu.make_async_copy(live_hbm, live_ref, scalar_sem.at[2]),
+    )
+    for copy in scalars:
+        copy.start()
     for i in range(steps):
         for copy in copies(i):
             copy.start()
-    acc_ref[...] = jnp.zeros_like(acc_ref)
+
+    part = rows * PIECES
+
+    def clear(k, carry):
+        acc_ref[pl.ds(pl.multiple_of(k * part, 8), part), :] = jnp.zeros((part, cells), jnp.float32)
+        return carry
+
+    lax.fori_loop(0, owners, clear, 0)
     tot[...] = jnp.zeros_like(tot)
     top[...] = jnp.zeros_like(top)
+    products[...] = jnp.zeros_like(products)
     extra = lax.broadcasted_iota(jnp.int32, (fx.shape[0] - field_count, fx.shape[1]), 0)
     fx[field_count:, :] = jnp.where(extra == 0, 1.0, 0.0)
+    for copy in scalars:
+        copy.wait()
     live = live_ref[0]
-    part = 16
+    place = lax.broadcasted_iota(jnp.int32, (GROUP, cells), 0)
+
+    def accumulate(first, half):
+        for j in range(GROUP):
+            b = first + j
+            owner, _ = split(slot_ref[b], capacity)
+            piece, target = split(target_ref[b], TILE)
+            row = (owner * PIECES + piece) * rows + target * (field_count + 1)
+            acc_ref[pl.ds(row, 16), :] += products[half, j * 16 : (j + 1) * 16, :]
 
     def step(i, carry):
         for copy in copies(i):
             copy.wait()
         fx[:field_count, :] = f_all[i].astype(jnp.float32)
+        keep = jnp.where(i * GROUP + place < live, m_all[i], 0).astype(jnp.float32)
         total = tot[...]
         most = top[...]
-        for first in range(0, GROUP, part):
-            products = []
-            for j in range(first, first + part):
-                b = i * GROUP + j
-                kept = jnp.where(b < live, m_all[i, j : j + 1, :], 0).astype(jnp.float32)
-                x = fx[:, j * cells : (j + 1) * cells] * kept
-                total = total + x
-                most = jnp.maximum(most, jnp.abs(x))
-                products.append(
-                    jnp.dot(x.astype(jnp.bfloat16), w_all[i, j], preferred_element_type=jnp.float32)
-                )
-            for j in range(first, first + part):
-                b = i * GROUP + j
-                target = target_ref[b]
-                row = ((slot_ref[b] // capacity) * PIECES + target // TILE) * rows
-                row = row + (target % TILE) * (field_count + 1)
-                acc_ref[pl.ds(row, 16), :] += products[j - first]
+        now = i & 1
+        for j in range(GROUP):
+            x = fx[:, j * cells : (j + 1) * cells] * keep[j : j + 1, :]
+            total = total + x
+            most = jnp.maximum(most, jnp.abs(x))
+            products[now, j * 16 : (j + 1) * 16, :] = jnp.dot(
+                x.astype(jnp.bfloat16), w_all[i, j], preferred_element_type=jnp.float32
+            )
+        accumulate(jnp.maximum(i - 1, 0) * GROUP, 1 - now)
         tot[...] = total
         top[...] = most
         return carry
 
     lax.fori_loop(0, steps, step, 0)
+    accumulate((steps - 1) * GROUP, (steps - 1) & 1)
     total = tot[...]
     most = top[...]
     low = jnp.sum(total[:TILE], axis=1, keepdims=True)
@@ -256,10 +282,9 @@
     capacity = max(2, 2 * block_count // owners)
     rows = (field_count + 2) * TILE
     steps = block_count // GROUP
-    smem = pl.BlockSpec(memory_space=pltpu.SMEM)
     acc = pl.pallas_call(
         functools.partial(contribute, capacity, rows, owners),
-        in_specs=[smem, smem, smem] + [pl.BlockSpec(memory_space=pltpu.HBM)] * 3,
+        in_specs=[pl.BlockSpec(memory_space=pl.ANY)] * 6,
         out_specs=pl.BlockSpec(memory_space=pltpu.VMEM),
         out_shape=jax.ShapeDtypeStruct((owners * PIECES * rows, cells), jnp.float32),
         scratch_shapes=[
@@ -267,9 +292,14 @@
             pltpu.VMEM((steps, GROUP, cells), jnp.int32),
             pltpu.VMEM((steps, GROUP, cells, cells), jnp.bfloat16),
             pltpu.VMEM((16, GROUP * cells), jnp.float32),
+            pltpu.VMEM((2, GROUP * 16, cells), jnp.float32),
             pltpu.VMEM((16, cells), jnp.float32),
             pltpu.VMEM((16, cells), jnp.float32),
+            pltpu.SMEM(send_slot.shape, jnp.int32),
+            pltpu.SMEM(target_block.shape, jnp.int32),
+            pltpu.SMEM(live_blocks.shape, jnp.int32),
             pltpu.SemaphoreType.DMA((3, steps)),
+            pltpu.SemaphoreType.DMA((3,)),
         ],
         compiler_params=pltpu.CompilerParams(
             vmem_limit_bytes=40 * 2**20

time: 35.5 us -> 34.7 us (0.977)
  Pallas kernels: 33.9 us -> 33.1 us
    pallas_call x1, Pallas kernels: 6.74 us -> 5.99 us  [body(): pl.pallas_call(functools.partial(contribute, capacity, rows, owners), in_...]
where the time goes in v1:
time: 34.7 us; the launch traced here: 34.5 us
  Pallas kernels  33.1 us (95%)
  local copies, waits for them, and re-layouts  0.71 us (2%)
  between operations  0.68 us (2%)
    pallas_call x1, Pallas kernels, body(): pl.pallas_call(functools.partial(exchange, sizes, orders, field_count), i...  27.1 us
    pallas_call x1, Pallas kernels, body(): pl.pallas_call(functools.partial(contribute, capacity, rows, owners), in_...  5.99 us
    unnamed x2, local copies, waits for them, and re-layouts  0.71 us

profile of v1, /device:TPU:0, one launch (start us, length us, event | category | flops | bytes accessed | tf_op | source)
XLA Modules:
  0.0 34.5 jit_solution(15926201550297540992)
XLA Ops:
  0.7 6.0 %shard_map.64 = f32[7168,128]{1,0:T(8,128)S(1)} custom-call(s32[256]{0:T(256)} %slot_hbm.1, s32[256]{0:T(256)} %target_hbm.1, s32[1]{0:T(128)S(6)} %copy.8.live_hbm, bf16[12,32768]{1,0:T(8,128)(2,1)} %f_hbm.1, s32[256,128]{1,0:T(8,128)} %bitcast.7, bf16[256,128,128]{2,1,0:T(8,128)(2,1)} %w_hbm.1), custom_call_target="tpu_custom_call" | custom-call | tf_op jit(solution)/shard_map/pallas_call | solution.py:285
  6.7 27.1 %shard_map.65 = f32[12,16,128]{2,1,0:T(8,128)S(1)} custom-call(f32[2,2,2,4,2,112,128]{6,5,4,3,2,1,0:T(8,128)S(1)} %bitcast.5), custom_call_target="tpu_custom_call" | custom-call | tf_op jit(solution)/shard_map/pallas_call | solution.py:337
  33.8 0.7 %copy.7 = f32[2,8,16,128]{3,1,2,0:T(8,128)} copy(f32[2,8,16,128]{3,2,1,0:T(8,128)S(1)} %bitcast.6) | data formatting | bytes 262144
  (1 shorter events, 0.0 us)

commit v2 on v1

v2 whole, which is shorter than its diff:
```python
import functools
import math

import jax
import jax.numpy as jnp
from jax import lax
from jax.experimental import pallas as pl
from jax.experimental.pallas import tpu as pltpu
from jax.sharding import PartitionSpec as P

TB_DEV = 16
GROUP = 16
TILE = 8
PIECES = TB_DEV // TILE
GAIN = 32700.0 / 6.0


def in_hbm(a):
    return pltpu.with_memory_space_constraint(a, pltpu.HBM)


def split(value, size):
    if size & (size - 1) == 0:
        return value >> (size.bit_length() - 1), value & (size - 1)
    return lax.div(value, size), lax.rem(value, size)


def contribute(
    capacity, owners, slot_hbm, target_hbm, live_hbm, f_hbm, m_hbm, w_hbm, acc_ref, tot_ref,
    f_all, m_all, w_all, fx, products, tot, slot_ref, target_ref, live_ref, sem, scalar_sem,
):
    field_count = f_hbm.shape[0]
    cells = w_hbm.shape[2]
    steps = f_all.shape[0]
    width = GROUP * cells

    def copies(i):
        return (
            pltpu.make_async_copy(m_hbm.at[pl.ds(i * GROUP, GROUP)], m_all.at[i], sem.at[0, i]),
            pltpu.make_async_copy(f_hbm.at[:, pl.ds(i * width, width)], f_all.at[i], sem.at[1, i]),
            pltpu.make_async_copy(w_hbm.at[pl.ds(i * GROUP, GROUP)], w_all.at[i], sem.at[2, i]),
        )

    scalars = (
        pltpu.make_async_copy(slot_hbm, slot_ref, scalar_sem.at[0]),
        pltpu.make_async_copy(target_hbm, target_ref, scalar_sem.at[1]),
        pltpu.make_async_copy(live_hbm, live_ref, scalar_sem.at[2]),
    )
    for copy in scalars:
        copy.start()
    for i in range(steps):
        for copy in copies(i):
            copy.start()

    stride = field_count + 1
    part = TB_DEV * stride

    def clear(k, carry):
        acc_ref[pl.ds(pl.multiple_of(k * part, 8), part), :] = jnp.zeros((part, cells), jnp.float32)
        return carry

    lax.fori_loop(0, owners, clear, 0)
    acc_ref[owners * part :, :] = jnp.zeros((TILE, cells), jnp.float32)
    tot[...] = jnp.zeros_like(tot)
    products[...] = jnp.zeros_like(products)
    extra = lax.broadcasted_iota(jnp.int32, (fx.shape[0] - field_count, fx.shape[1]), 0)
    fx[field_count:, :] = jnp.where(extra == 0, 1.0, 0.0)
    for copy in scalars:
        copy.wait()
    live = live_ref[0]
    place = lax.broadcasted_iota(jnp.int32, (GROUP, cells), 0)

    def accumulate(first, half):
        for j in range(GROUP):
            b = first + j
            owner, _ = split(slot_ref[b], capacity)
            row = (owner * TB_DEV + target_ref[b]) * stride
            acc_ref[pl.ds(row, 16), :] += products[half, j * 16 : (j + 1) * 16, :]

    def step(i, carry):
        for copy in copies(i):
            copy.wait()
        accumulate(jnp.maximum(i - 1, 0) * GROUP, (i + 1) & 1)
        fx[:field_count, :] = f_all[i].astype(jnp.float32)
        keep = jnp.where(i * GROUP + place < live, m_all[i], 0).astype(jnp.float32)
        total = tot[...]
        now = i & 1
        for j in range(GROUP):
            x = fx[:, j * cells : (j + 1) * cells] * keep[j : j + 1, :]
            total = total + x
            products[now, j * 16 : (j + 1) * 16, :] = jnp.dot(
                x.astype(jnp.bfloat16), w_all[i, j], preferred_element_type=jnp.float32
            )
        tot[...] = total
        return carry

    lax.fori_loop(0, steps, step, 0)
    accumulate((steps - 1) * GROUP, (steps - 1) & 1)
    total = tot[...]
    low = jnp.sum(total[:TILE], axis=1, keepdims=True)
    high = jnp.sum(total[TILE:], axis=1, keepdims=True)
    lane = lax.broadcasted_iota(jnp.int32, (TILE, cells), 1)
    tot_ref[...] = jnp.where(lane == 0, low, high)


def exchange(sizes, field_count, acc_ref, tot_ref, out_ref, *scratch):
    ny, nx, nz = sizes["y"], sizes["x"], sizes["z"]
    band, z = lax.axis_index("band"), lax.axis_index("sub")
    core = lax.rem(band, 2)
    x = lax.rem(band // 2, nx)
    y = band // (2 * nx)
    stride = field_count + 1
    span = TB_DEV * stride
    cells = acc_ref.shape[-1]

    def device(y, x, core, z):
        return {"band": (y * nx + x) * 2 + core, "sub": z}

    near = [(dy, dx) for dy in range(ny) for dx in range(nx)]
    near.sort(key=lambda d: -(d[0] > 0) - (d[1] > 0))
    peers = near[:-1]

    def chip(k):
        dy, dx = near[k]
        return lax.rem(y + dy, ny), lax.rem(x + dx, nx)

    def along(j):
        if j == nz - 1:
            return z
        high = (2 * z) // nz
        down = nz - 1 - j
        down = down - (z - down + nz) // nz
        up = j + (j - z + nz) // nz
        return (1 - high) * down + high * up

    partners = [device(y, x, 1 - core, z)]
    partners += [device(*chip(k), core, z) for k in range(len(peers))]
    partners += [device(y, x, core, lax.rem(z + k, nz)) for k in range(1, nz)]
    barrier = pltpu.get_barrier_semaphore()
    for partner in partners:
        pl.semaphore_signal(barrier, inc=1, device_id=partner, device_id_type=pl.DeviceIdType.MESH)
    pl.semaphore_wait(barrier, len(partners))

    (landed, out_codes, out_heads, in_codes, in_heads, far_codes, far_heads, got_codes, got_heads,
     sums, result, chip_tot, near_tot, plane_tot, far_tot, send_sem, recv_sem) = scratch
    counter = [0]
    started = []

    def claim(count=1):
        counter[0] += count
        return counter[0] - count

    def send(src, dst, partner, slot=None):
        k = claim()
        copy = pltpu.make_async_remote_copy(
            src_ref=src,
            dst_ref=dst,
            send_sem=send_sem.at[k],
            recv_sem=recv_sem.at[k if slot is None else slot],
            device_id=partner,
            device_id_type=pl.DeviceIdType.MESH,
        )
        copy.start()
        started.append(copy)
        return copy

    def first_row(k, j, core):
        at = device(*chip(k), core, along(j))
        return pl.multiple_of((at["band"] * nz + at["sub"]) * span, 8)

    def encode(load, fraction, codes, heads, at):
        gain = jnp.where(fraction > 0.0, GAIN / fraction, 0.0)
        for f in range(0, field_count, 2):
            pair = jnp.concatenate([load(f) * gain, load(f + 1) * gain], axis=0)
            codes[(*at, slice(f * TILE, (f + 2) * TILE))] = jnp.round(pair).astype(jnp.int32).astype(jnp.int16)
        heads[at] = fraction

    def decode(codes, gain, at, f):
        pair = codes[(*at, slice(f * TILE, (f + 2) * TILE))].astype(jnp.int32).astype(jnp.float32)
        return pair[:TILE] * gain, pair[TILE:] * gain

    own = len(peers)
    partner = device(y, x, 1 - core, z)
    merges = {}
    tot_copy = send(tot_ref, chip_tot.at[0], partner)
    for j in range(nz):
        for k in range(own + 1):
            rows = pl.ds(first_row(k, j, 1 - core), span)
            merges[j, k] = send(acc_ref.at[rows], landed.at[j, k], partner)

    def merged(j, k, p):
        start = first_row(k, j, core) + p * TILE * stride

        def load(f):
            there = landed[j, k, pl.ds(p * TILE * stride + f, TILE, stride=stride), :]
            return acc_ref[pl.ds(start + f, TILE, stride=stride), :] + there

        return load

    spreads = {}
    for j in range(nz):
        for k in range(own):
            merges[j, k].wait_recv()
            for p in range(PIECES):
                load = merged(j, k, p)
                encode(load, load(field_count), out_codes, out_heads, (j, k, p))
            to = device(*chip(k), core, z)
            spreads[j, k] = (
                send(out_codes.at[j, k], in_codes.at[j, k], to),
                send(out_heads.at[j, k], in_heads.at[j, k], to),
            )
    tot_copy.wait_recv()
    chip_tot[1] = tot_ref[...] + chip_tot[0]
    near_copies = [
        send(chip_tot.at[1], near_tot.at[k], device(*chip(k), core, z)) for k in range(own)
    ]

    far_slots = claim(3 * (nz - 1))
    far_copies = []
    for j in range(nz):
        merges[j, own].wait_recv()
        for k in range(own):
            for copy in spreads[j, k]:
                copy.wait_recv()
        for p in range(PIECES):
            load = merged(j, own, p)
            heads = [in_heads[j, k, p] for k in range(own)]
            gains = [head * (1.0 / GAIN) for head in heads]
            fraction = functools.reduce(jnp.add, heads, load(field_count))
            scale = None
            if j < nz - 1:
                scale = jnp.where(fraction > 0.0, GAIN / fraction, 0.0)
            for f in range(0, field_count, 2):
                first, second = load(f), load(f + 1)
                for k in range(own):
                    a, b = decode(in_codes, gains[k], (j, k, p), f)
                    first, second = first + a, second + b
                if scale is None:
                    sums[p, f * TILE : (f + 1) * TILE] = first
                    sums[p, (f + 1) * TILE : (f + 2) * TILE] = second
                else:
                    pair = jnp.concatenate([first * scale, second * scale], axis=0)
                    code = jnp.round(pair).astype(jnp.int32).astype(jnp.int16)
                    far_codes[j, p, f * TILE : (f + 2) * TILE] = code
            if scale is None:
                sums[p, field_count * TILE : (field_count + 1) * TILE] = fraction
            else:
                far_heads[j, p] = fraction
        if j < nz - 1:
            zj = along(j)
            slot = lax.rem(zj - z + nz, nz) - 1
            to = device(y, x, core, zj)
            send(far_codes.at[j], got_codes.at[slot], to, far_slots + 3 * slot)
            send(far_heads.at[j], got_heads.at[slot], to, far_slots + 3 * slot + 1)
        if j == 0:
            total = chip_tot[1]
            for k, copy in enumerate(near_copies):
                copy.wait_recv()
                total = total + near_tot[k]
            plane_tot[...] = total
            for k in range(1, nz):
                to = device(y, x, core, lax.rem(z + k, nz))
                send(plane_tot, far_tot.at[k - 1], to, far_slots + 3 * (k - 1) + 2)

    total = plane_tot[...]
    for k in range(nz - 1):
        for src, dst, which in (
            (far_codes.at[k], got_codes.at[k], 0),
            (far_heads.at[k], got_heads.at[k], 1),
            (plane_tot, far_tot.at[k], 2),
        ):
            pltpu.make_async_remote_copy(
                src_ref=src,
                dst_ref=dst,
                send_sem=send_sem.at[0],
                recv_sem=recv_sem.at[far_slots + 3 * k + which],
                device_id=device(y, x, core, lax.rem(z + k + 1, nz)),
                device_id_type=pl.DeviceIdType.MESH,
            ).wait_recv()
        total = total + far_tot[k]
    row, column = field_count % TILE, field_count // TILE
    means = total / jnp.maximum(total[row : row + 1, column : column + 1], 1.0)
    for p in range(PIECES):
        heads = [got_heads[k, p] for k in range(nz - 1)]
        gains = [head * (1.0 / GAIN) for head in heads]
        own_fraction = sums[p, field_count * TILE : (field_count + 1) * TILE]
        fraction = functools.reduce(jnp.add, heads, own_fraction)
        short = jnp.maximum(0.25 - fraction, 0.0)
        least = 1.0 / jnp.maximum(fraction, 0.25)
        for f in range(0, field_count, 2):
            tiles = [sums[p, (f + i) * TILE : (f + i + 1) * TILE] for i in range(2)]
            for k in range(nz - 1):
                tiles = [a + b for a, b in zip(tiles, decode(got_codes, gains[k], (k, p), f))]
            for i in range(2):
                row, column = (f + i) % TILE, (f + i) // TILE
                mean = means[row : row + 1, column : column + 1]
                start = (f + i) * TB_DEV + p * TILE
                result[start : start + TILE] = (tiles[i] + short * mean) * least
    for t in range(TB_DEV):
        columns = result[pl.ds(t, field_count, stride=TB_DEV), :]
        out_ref[:, t * cells : (t + 1) * cells] = columns
    for copy in started:
        copy.wait_send()


def body(sizes, fields, land_mask, intersection, send_slot, target_block, live_blocks):
    block_count, cells = intersection.shape[0], intersection.shape[1]
    field_count = fields.shape[0]
    nx, ny, nz = sizes["x"], sizes["y"], sizes["z"]
    owners = ny * nx * 2 * nz
    capacity = max(2, 2 * block_count // owners)
    stride = field_count + 1
    span = TB_DEV * stride
    steps = block_count // GROUP
    vmem = pl.BlockSpec(memory_space=pltpu.VMEM)
    acc, tot = pl.pallas_call(
        functools.partial(contribute, capacity, owners),
        in_specs=[pl.BlockSpec(memory_space=pl.ANY)] * 6,
        out_specs=[vmem, vmem],
        out_shape=[
            jax.ShapeDtypeStruct((owners * span + TILE, cells), jnp.float32),
            jax.ShapeDtypeStruct((TILE, cells), jnp.float32),
        ],
        scratch_shapes=[
            pltpu.VMEM((steps, field_count, GROUP * cells), jnp.bfloat16),
            pltpu.VMEM((steps, GROUP, cells), jnp.int32),
            pltpu.VMEM((steps, GROUP, cells, cells), jnp.bfloat16),
            pltpu.VMEM((16, GROUP * cells), jnp.float32),
            pltpu.VMEM((2, GROUP * 16, cells), jnp.float32),
            pltpu.VMEM((16, cells), jnp.float32),
            pltpu.SMEM(send_slot.shape, jnp.int32),
            pltpu.SMEM(target_block.shape, jnp.int32),
            pltpu.SMEM(live_blocks.shape, jnp.int32),
            pltpu.SemaphoreType.DMA((3, steps)),
            pltpu.SemaphoreType.DMA((3,)),
        ],
        compiler_params=pltpu.CompilerParams(
            vmem_limit_bytes=40 * 2**20
        ),
    )(
        in_hbm(send_slot),
        in_hbm(target_block),
        live_blocks,
        in_hbm(fields),
        in_hbm(land_mask.reshape(block_count, cells)),
        in_hbm(intersection),
    )

    plane = ny * nx
    code, head = (PIECES, field_count * TILE, cells), (PIECES, TILE, cells)
    near, far = (nz, plane - 1), (nz - 1,)
    copies = 1 + nz * plane + (plane - 1) * (2 * nz + 1) + 6 * (nz - 1)
    return pl.pallas_call(
        functools.partial(exchange, sizes, field_count),
        in_specs=[vmem, vmem],
        out_specs=vmem,
        out_shape=jax.ShapeDtypeStruct((field_count, TB_DEV * cells), jnp.float32),
        scratch_shapes=[
            pltpu.VMEM((nz, plane, span, cells), jnp.float32),
            pltpu.VMEM((*near, *code), jnp.int16),
            pltpu.VMEM((*near, *head), jnp.float32),
            pltpu.VMEM((*near, *code), jnp.int16),
            pltpu.VMEM((*near, *head), jnp.float32),
            pltpu.VMEM((*far, *code), jnp.int16),
            pltpu.VMEM((*far, *head), jnp.float32),
            pltpu.VMEM((*far, *code), jnp.int16),
            pltpu.VMEM((*far, *head), jnp.float32),
            pltpu.VMEM((PIECES, stride * TILE, cells), jnp.float32),
            pltpu.VMEM((field_count * TB_DEV, cells), jnp.float32),
            pltpu.VMEM((2, TILE, cells), jnp.float32),
            pltpu.VMEM((plane - 1, TILE, cells), jnp.float32),
            pltpu.VMEM((TILE, cells), jnp.float32),
            pltpu.VMEM((nz - 1, TILE, cells), jnp.float32),
            pltpu.SemaphoreType.DMA((copies,)),
            pltpu.SemaphoreType.DMA((copies,)),
        ],
        compiler_params=pltpu.CompilerParams(
            collective_id=0, has_side_effects=True, vmem_limit_bytes=50 * 2**20
        ),
    )(acc, tot)


def solution(mesh):
    band, sub = mesh.shape["band"], mesh.shape["sub"]
    plane = band // 2
    nx = max(d for d in range(1, math.isqrt(plane) + 1) if plane % d == 0)
    sizes = {"y": plane // nx, "x": nx, "z": sub}
    return jax.shard_map(
        functools.partial(body, sizes),
        mesh=mesh,
        in_specs=(
            P(None, ("band", "sub")),
            P(("band", "sub")),
            P(("band", "sub"), None, None),
            P(("band", "sub")),
            P(("band", "sub")),
            P(("band", "sub")),
        ),
        out_specs=P(None, ("band", "sub")),
        check_vma=False,
    )
```

time: 34.7 us -> 31.1 us (0.90)
  Pallas kernels: 33.1 us -> 29.6 us
    pallas_call x2, Pallas kernels: 33.1 us -> 29.6 us  [the longest x1 23.8 us: body(): pl.pallas_call(functools.partial(exchange, sizes, field_count), in_specs=...]
    unnamed x2 -> x1, local copies, waits for them, and re-layouts: 0.71 us -> 0.66 us
where the time goes in v2:
time: 31.1 us; the launch traced here: 31 us
  Pallas kernels  29.6 us (95%)
  between operations  0.67 us (2%)
  local copies, waits for them, and re-layouts  0.66 us (2%)
    pallas_call x1, Pallas kernels, body(): pl.pallas_call(functools.partial(exchange, sizes, field_count), in_specs=...  23.8 us
    pallas_call x1, Pallas kernels, body(): pl.pallas_call(functools.partial(contribute, capacity, owners), in_specs=...  5.86 us
    unnamed x1, local copies, waits for them, and re-layouts  0.66 us

profile of v2, /device:TPU:0, one launch (start us, length us, event | category | flops | bytes accessed | tf_op | source)
XLA Modules:
  0.0 31.0 jit_solution(1943669071889593882)
XLA Ops:
  0.7 5.9 %shard_map.64 = (f32[6664,128]{1,0:T(8,128)S(1)}, f32[8,128]{1,0:T(8,128)S(1)}) custom-call(s32[256]{0:T(256)} %slot_hbm.1, s32[256]{0:T(256)} %target_hbm.1, s32[1]{0:T(128)S(6)} %copy.8.live_hbm, bf16[12,32768]{1,0:T(8,128)(2,1)} %f_hbm.1, s32[256,128]{1,0:T(8,128)} %bitcast.1, bf16[256,128,128]{2,1,0:T(8,128)(2,1)} %w_hbm.1), custom_call_target="tpu_custom_call" | custom-call | tf_op jit(solution)/shard_map/pallas_call | solution.py:316
  6.5 23.8 %shard_map.65 = f32[12,2048]{1,0:T(8,128)S(1)} custom-call(f32[6664,128]{1,0:T(8,128)S(1)} %get-tuple-element.7.acc_ref, f32[8,128]{1,0:T(8,128)S(1)} %get-tuple-element.8.tot_ref), custom_call_target="tpu_custom_call" | custom-call | tf_op jit(solution)/shard_map/pallas_call | solution.py:353
  30.3 0.7 %copy.9 = f32[12,2048]{1,0:T(8,128)} copy(f32[12,2048]{1,0:T(8,128)S(1)} %shard_map.65) | data formatting | bytes 196608
